TPU v7x, 32 devices: a whole 2x2x4 slice. The times are simulated.
32 devices in a mesh: row: 4 (over y, x), rhs: 8 (over z, core).
Axes of the slice: x: 2, y: 2, z: 4, core: 2. Of those that a mesh axis runs over, the one named last changes fastest.
Arguments:
- factor: float32 [3072, 12, 256], P('row', None, 'rhs'), as said below
- inverses: float32 [12, 256, 256], P('row'), as said below
- right_side: float32 [3072, 4096], P('row', 'rhs'), may hold values from -6 to 6
Outputs:
- solution: float32 [3072, 4096], P('row', 'rhs')
Inputs may be any that keep to these rules, and one draw needn't show every extreme that they name: factor[i, j, c] is zero unless j is less than i // 256. Each inverses[p] is lower triangular with a positive diagonal.
All inputs are finite; a program needn't handle non-finite values.
Results may differ from a plain program's by a relative error of at most 0.0001.
Values sent between devices are 32-bit elements; how exact they have to be, the bound alone decides.
No kernel may reach another device: no remote copies, remote signals or barrier semaphores. Data moves between devices by JAX's collectives and lax.ppermute only.
A program may use at most 128 MiB of HBM per device.

v0:
```python
import jax
import jax.numpy as jnp
from jax import lax
from jax.sharding import PartitionSpec as P


def from_root(block, axis, owner):
    block = jnp.where(lax.axis_index(axis) == owner, block, jnp.zeros_like(block))
    return lax.psum(block, axis)


def mult(left, right):
    return jnp.dot(left, right, preferred_element_type=jnp.float32, precision=lax.Precision.HIGHEST)


def body(factor, inverses, right_side):
    block = right_side.shape[0]
    panel = inverses.shape[1]
    per_block = inverses.shape[0]
    rounds = lax.axis_size("row")
    mine = lax.axis_index("row")
    gathered = lax.all_gather(factor, "rhs", axis=2, tiled=True)

    def fetch(first, count):
        return lax.dynamic_slice_in_dim(gathered, first, count, 1)

    def apply_tiles(residual, tiles, solved):
        return residual - mult(tiles.reshape(block, -1), solved)

    solution = jnp.zeros_like(right_side)

    def step_block(index, state):
        residual, solution = state
        tiles = fetch(index * per_block, per_block)
        working = residual
        pieces = []
        for inner in range(per_block):
            solved_part = mult(inverses[inner], working[inner * panel : (inner + 1) * panel])
            pieces.append(solved_part)
            working = working - mult(tiles[:, inner, :], solved_part)
        solved = from_root(jnp.concatenate(pieces, axis=0), "row", index)
        residual = apply_tiles(residual, tiles, solved)
        solution = jnp.where(mine == index, solved, solution)
        return (residual, solution)

    residual, solution = lax.fori_loop(0, rounds, step_block, (right_side, solution))
    return solution


def solution(mesh):
    placed = (P("row", None, "rhs"), P("row", None, None), P("row", "rhs"))
    return jax.shard_map(
        body, mesh=mesh, in_specs=placed, out_specs=P("row", "rhs"), check_vma=False
    )
```

profile of v0, /device:TPU:0, one launch (start us, length us, event | category | flops | bytes accessed | tf_op | source)
XLA Modules:
  0.0 417.8 jit_solution(4897587918877244173)
XLA Ops:
  6.5 0.7 all-gather.2.cloned.1.call-update
  7.3 95.1 %all-gather.2.cloned.1.call-done = f32[768,12,256]{0,2,1:T(8,128)} async-done(((f32[768,12,32]{0,2,1:T(8,128)}), f32[768,12,256]{0,2,1:T(8,128)}) %all-gather.2.cloned.1.call-update) | async-done | bytes 9437200 | tf_op jit(solution)/shard_map/all_gather | solution.py:22
  102.4 307.8 %while.16 = (s32[]{:T(128)}, f32[768,512]{1,0:T(8,128)S(1)}, f32[768,512]{1,0:T(8,128)S(1)}, f32[768,12,256]{0,2,1:T(8,128)}, f32[3,256,256]{2,1,0:T(8,128)}, /*...) while((s32[]{:T(128)}, f32[768,512]{1,0:T(8,128)S(1)}, ...), condition=%wide.region_2.3_spmd.clone, body=%wide.region_0.2_spmd.clone.sunk | while | flops 7251034112 | bytes 50332000 | solution.py:46
  102.4 1.6 fusion.39
  104.0 2.7 convolution_subtract_fusion.4
  106.7 0.6 fusion.40
  107.3 2.6 fusion.41
  109.9 0.7 convolution_bitcast_fusion.2
  110.6 1.3 maximum_select_fusion.2
  111.9 3.2 constant_dynamic-slice_fusion.2
  115.1 56.1 %all-reduce.2.cloned.1.call-done = f32[768,512]{1,0:T(8,128)} async-done(((f32[768,512]{1,0:T(8,128)}), f32[768,512]{1,0:T(8,128)}) %all-reduce.2.cloned.1.call-update) | async-done | bytes 1572880 | tf_op jit(solution)/shard_map/while/body/eval_jaxpr/psum | solution.py:9
  171.2 6.4 %convolution_subtract_fusion.5 = f32[768,512]{1,0:T(8,128)S(1)} fusion(f32[768,512]{1,0:T(8,128)S(1)} %get-tuple-element.198, f32[768,768]{0,1:T(8,128)} %bitcast.47, f32[768,512]{1,0:T(8,128)} %all-reduce.2.cloned.1.call-done), kind=kOutput, calls=%fused_computation.3.clone.1 | convolution fusion | flops 3624271872 | bytes 7077888 | tf_op jit(solution)/shard_map/while/body/eval_jaxpr/dot_general | solution.py:13
  177.6 0.5 select_select_fusion.2
  178.1 0.0 all-reduce.2.cloned.1.call-start
  178.2 1.6 fusion.39
  179.8 2.7 convolution_subtract_fusion.4
  182.4 0.6 fusion.40
  183.1 2.6 fusion.41
  185.7 0.7 convolution_bitcast_fusion.2
  186.3 1.3 maximum_select_fusion.2
  187.6 0.0 all-reduce.2.cloned.1.call-update
  187.7 3.2 constant_dynamic-slice_fusion.2
  190.9 57.7 %all-reduce.2.cloned.1.call-done = f32[768,512]{1,0:T(8,128)} async-done(((f32[768,512]{1,0:T(8,128)}), f32[768,512]{1,0:T(8,128)}) %all-reduce.2.cloned.1.call-update) | async-done | bytes 1572880 | tf_op jit(solution)/shard_map/while/body/eval_jaxpr/psum | solution.py:9
  248.5 6.4 %convolution_subtract_fusion.5 = f32[768,512]{1,0:T(8,128)S(1)} fusion(f32[768,512]{1,0:T(8,128)S(1)} %get-tuple-element.198, f32[768,768]{0,1:T(8,128)} %bitcast.47, f32[768,512]{1,0:T(8,128)} %all-reduce.2.cloned.1.call-done), kind=kOutput, calls=%fused_computation.3.clone.1 | convolution fusion | flops 3624271872 | bytes 7077888 | tf_op jit(solution)/shard_map/while/body/eval_jaxpr/dot_general | solution.py:13
  255.0 0.5 select_select_fusion.2
  255.5 0.0 all-reduce.2.cloned.1.call-start
  255.5 1.6 fusion.39
  257.1 2.7 convolution_subtract_fusion.4
  259.8 0.6 fusion.40
  260.4 2.6 fusion.41
  263.0 0.7 convolution_bitcast_fusion.2
  263.7 1.3 maximum_select_fusion.2
  265.0 3.2 constant_dynamic-slice_fusion.2
  268.2 57.7 %all-reduce.2.cloned.1.call-done = f32[768,512]{1,0:T(8,128)} async-done(((f32[768,512]{1,0:T(8,128)}), f32[768,512]{1,0:T(8,128)}) %all-reduce.2.cloned.1.call-update) | async-done | bytes 1572880 | tf_op jit(solution)/shard_map/while/body/eval_jaxpr/psum | solution.py:9
  325.9 6.4 %convolution_subtract_fusion.5 = f32[768,512]{1,0:T(8,128)S(1)} fusion(f32[768,512]{1,0:T(8,128)S(1)} %get-tuple-element.198, f32[768,768]{0,1:T(8,128)} %bitcast.47, f32[768,512]{1,0:T(8,128)} %all-reduce.2.cloned.1.call-done), kind=kOutput, calls=%fused_computation.3.clone.1 | convolution fusion | flops 3624271872 | bytes 7077888 | tf_op jit(solution)/shard_map/while/body/eval_jaxpr/dot_general | solution.py:13
  332.3 0.5 select_select_fusion.2
  332.8 0.0 all-reduce.2.cloned.1.call-start
  332.9 1.6 fusion.39
  334.5 2.7 convolution_subtract_fusion.4
  337.1 0.6 fusion.40
  337.8 2.6 fusion.41
  340.4 0.7 convolution_bitcast_fusion.2
  341.0 1.3 maximum_select_fusion.2
  342.4 3.2 constant_dynamic-slice_fusion.2
  345.6 57.7 %all-reduce.2.cloned.1.call-done = f32[768,512]{1,0:T(8,128)} async-done(((f32[768,512]{1,0:T(8,128)}), f32[768,512]{1,0:T(8,128)}) %all-reduce.2.cloned.1.call-update) | async-done | bytes 1572880 | tf_op jit(solution)/shard_map/while/body/eval_jaxpr/psum | solution.py:9
  403.3 6.4 %convolution_subtract_fusion.5 = f32[768,512]{1,0:T(8,128)S(1)} fusion(f32[768,512]{1,0:T(8,128)S(1)} %get-tuple-element.198, f32[768,768]{0,1:T(8,128)} %bitcast.47, f32[768,512]{1,0:T(8,128)} %all-reduce.2.cloned.1.call-done), kind=kOutput, calls=%fused_computation.3.clone.1 | convolution fusion | flops 3624271872 | bytes 7077888 | tf_op jit(solution)/shard_map/while/body/eval_jaxpr/dot_general | solution.py:13
  409.7 0.5 select_select_fusion.2
  410.2 1.1 copy-done.2
  (25 shorter events, 0.1 us)
Async XLA Ops:
  6.5 95.9 %copy-start = (f32[768,512]{1,0:T(8,128)S(1)}, f32[768,512]{1,0:T(8,128)}, u32[]{:S(2)}) copy-start(f32[768,512]{1,0:T(8,128)} %param.7) | copy-start | bytes 4718596
  6.5 95.9 %all-gather.2.cloned.1.call-start = ((), (), s32[]{:S(2)}) async-start(), calls=%async_computation | async-start | bytes 10616832 | tf_op jit(solution)/shard_map/all_gather | solution.py:22
  102.4 68.8 %all-reduce.2.cloned.1.call-start = ((), (), s32[]{:S(2)}) async-start(), calls=%async_computation.1 | async-start | bytes 3145728 | tf_op jit(solution)/shard_map/while/body/eval_jaxpr/psum | solution.py:9
  104.0 2.7 copy-start.3
  171.2 6.4 %copy-start.1 = (f32[768,512]{1,0:T(8,128)S(1)}, f32[768,512]{1,0:T(8,128)}, u32[]{:S(2)}) copy-start(f32[768,512]{1,0:T(8,128)} %all-reduce.2.cloned.1.call-done) | copy-start | bytes 4718596 | tf_op jit(solution)/shard_map/while
  178.1 70.4 %all-reduce.2.cloned.1.call-start = ((), (), s32[]{:S(2)}) async-start(), calls=%async_computation.1 | async-start | bytes 3145728 | tf_op jit(solution)/shard_map/while/body/eval_jaxpr/psum | solution.py:9
  179.7 2.7 copy-start.3
  248.5 6.4 %copy-start.1 = (f32[768,512]{1,0:T(8,128)S(1)}, f32[768,512]{1,0:T(8,128)}, u32[]{:S(2)}) copy-start(f32[768,512]{1,0:T(8,128)} %all-reduce.2.cloned.1.call-done) | copy-start | bytes 4718596 | tf_op jit(solution)/shard_map/while
  255.5 70.4 %all-reduce.2.cloned.1.call-start = ((), (), s32[]{:S(2)}) async-start(), calls=%async_computation.1 | async-start | bytes 3145728 | tf_op jit(solution)/shard_map/while/body/eval_jaxpr/psum | solution.py:9
  257.1 2.7 copy-start.3
  325.9 6.4 %copy-start.1 = (f32[768,512]{1,0:T(8,128)S(1)}, f32[768,512]{1,0:T(8,128)}, u32[]{:S(2)}) copy-start(f32[768,512]{1,0:T(8,128)} %all-reduce.2.cloned.1.call-done) | copy-start | bytes 4718596 | tf_op jit(solution)/shard_map/while
  332.8 70.4 %all-reduce.2.cloned.1.call-start = ((), (), s32[]{:S(2)}) async-start(), calls=%async_computation.1 | async-start | bytes 3145728 | tf_op jit(solution)/shard_map/while/body/eval_jaxpr/psum | solution.py:9
  334.5 2.7 copy-start.3
  403.3 6.4 %copy-start.1 = (f32[768,512]{1,0:T(8,128)S(1)}, f32[768,512]{1,0:T(8,128)}, u32[]{:S(2)}) copy-start(f32[768,512]{1,0:T(8,128)} %all-reduce.2.cloned.1.call-done) | copy-start | bytes 4718596 | tf_op jit(solution)/shard_map/while
  410.2 1.1 copy-start.2
Sparse Core Ops, SparseCore 0:
  8.9 93.4 all-gather.1
  112.0 59.1 all-reduce.1
  187.8 60.7 all-reduce.1
  265.1 60.7 all-reduce.1
  342.5 60.7 all-reduce.1
where the time goes:
time: 418 us
  waiting for transfers between devices  325 us (78%)
  matrix products  58 us (14%)
  local copies, waits for them, and re-layouts  14 us (3%)
  between operations  13.1 us (3%)
  other arithmetic  7.15 us (2%)
    psum x4, waiting for transfers between devices, from_root(): return lax.psum(block, axis)  229 us
    all_gather x1, waiting for transfers between devices, body(): gathered = lax.all_gather(factor, 'rhs', axis=2, tiled=True)  95.1 us
    dot_general x24, matrix products, mult(): jnp.dot(left, right, preferred_element_type=jnp.float32, precision=lax.Pr...  58 us
    dynamic_slice x4, local copies, waits for them, and re-layouts, fetch(): return lax.dynamic_slice_in_dim(gathered, first, count, 1)  12.8 us
  transfers between devices with their start and end apart: 5, of which 5 were waited for; matrix products, arithmetic and copies ran while one was open for 3% of the time, Pallas kernels for 0%

commit v1 on v0

v1 whole, which is shorter than its diff:
```python
import functools

import jax
import jax.numpy as jnp
from jax import lax
from jax.experimental import pallas as pl
from jax.experimental.pallas import tpu as pltpu
from jax.sharding import PartitionSpec as P


CHUNKS = 4
LAG = 2
GRANT = 20 * 1024 * 1024


def halves(value):
    high = value.astype(jnp.bfloat16)
    low = (value - high.astype(jnp.float32)).astype(jnp.bfloat16)
    return high, low


def times(left, high, low, contract=0):
    dims = (((1,), (contract,)), ((), ()))
    left_high, left_low = halves(left)
    dot = functools.partial(lax.dot_general, dimension_numbers=dims, preferred_element_type=jnp.float32)
    return dot(left_high, high) + (dot(left_low, high) + dot(left_high, low))


def prepare_kernel(masks, place, *refs):
    *parts, swapped, high, low = refs
    width = swapped.shape[2]
    for step, (mask, part) in enumerate(zip(masks, parts)):
        source = place[0] ^ mask
        for spot, value in ((source, part[...]), (source ^ 1, swapped[step])):
            first, second = halves(value)
            spot = pl.multiple_of(spot * width, width)
            high[:, pl.ds(spot, width), :] = first
            low[:, pl.ds(spot, width), :] = second


def turn_kernel(value, out):
    out[...] = value[...].T


def split_kernel(value, high, low):
    high[...], low[...] = halves(value[...])


def solve_into(out, inv_high, inv_low, low_high, low_low):
    count, panel, _ = inv_high.shape
    for p in range(count):
        here = slice(p * panel, (p + 1) * panel)
        solved = times(out[:, here], inv_high[p], inv_low[p], 1)
        out[:, here] = solved
        if p + 1 < count:
            rest = slice((p + 1) * panel, count * panel)
            tiles = (here, slice(p * panel, (count - 1) * panel))
            out[:, rest] -= times(solved, low_high[tiles], low_low[tiles])


def solve_kernel(layout, place, residual, *refs):
    *inputs, out = refs
    names, jobs, finish = layout
    at = dict(zip(names, inputs))
    rows = out.shape[0]
    for row, first, base, terms in jobs:

        @pl.when(place[0] == row)
        def _():
            out[...] = residual[first : first + rows, :] if base is None else at[base][...]
            for spot, key, offset, length, pair in terms:
                here = slice(spot, spot + length)
                solved = at[key][offset : offset + length, :]
                out[here, :] -= times(solved, at[pair + ("high",)][...], at[pair + ("low",)][...])
            if finish:
                solve_into(out, at["inv_high"], at["inv_low"], at["own", "high"], at["own", "low"])


def stack_kernel(*refs):
    *inputs, out = refs
    for step, value in enumerate(inputs):
        out[step] = value[...]


def join_kernel(*refs):
    *inputs, out = refs
    rows = inputs[0].shape[0]
    for step, value in enumerate(inputs):
        out[step * rows : (step + 1) * rows, :] = value[...]


def place_kernel(names, segments, place, *refs):
    *inputs, out, stage, sems = refs
    at = dict(zip(names, inputs))
    for row, parts in enumerate(segments):

        @pl.when(place[0] == row)
        def _():
            copies = []
            for step, (first, length, key) in enumerate(parts):
                copies.append(pltpu.make_async_copy(at[key], stage.at[pl.ds(first, length)], sems.at[step]))
                copies[-1].start()
            for copy in copies:
                copy.wait()

    out[...] = stage[...].T


class Plan:
    def __init__(self, rows, lanes):
        self.rows, self.lanes, self.last = rows, lanes, rows - 1
        self.steps = []
        self.arrived = {}
        self.solved = {row: [] for row in range(rows)}
        if rows == 4:
            self.four()
        else:
            self.many()

    def add(self, *step):
        if step not in self.steps:
            self.steps.append(step)
        return step

    def reach(self, name, *levels):
        count = self.lanes.bit_length() - 2
        for level in levels or range(count):
            bit = self.lanes >> (level + 1)
            for index in range(1 << level):
                self.add("z", name, bit, index)

    def pack(self, name):
        for kind in ("stack", "swap", "prepare"):
            self.add(kind, name)

    def solve(self, *units, base=None, done=(), only=None):
        jobs = []
        for row, first, count in units:
            owners = range(row) if only is None else only
            terms = []
            for owner in owners:
                if owner in done:
                    continue
                chunk = first
                while chunk < first + count:
                    key, start, length = self.arrived[row, owner, chunk]
                    length = min(length - (chunk - start), first + count - chunk)
                    terms.append((chunk - first, key, chunk - start, length, row - owner))
                    chunk += length
            jobs.append((row, first, tuple(terms)))
        key = self.add("solve", units[0][2], tuple(jobs), base, only is None)
        if only is None:
            for row, first, count in units:
                self.solved[row].append((first, count, key))
        return key

    def join(self, *keys):
        return self.add("join", *keys)

    def send(self, value, *moves):
        key = self.add("send", value, tuple((a, b) for a, b, *_ in moves))
        for _, target, owner, first, count in moves:
            for chunk in range(first, first + count):
                self.arrived[target, owner, chunk] = (key, first, count)
        return key

    def four(self):
        half = CHUNKS // 2
        self.reach(0, 0)
        self.add("z", 0, 2, 0)
        self.add("turn")
        self.add("split")
        self.add("z", 0, 2, 1)
        self.add("stack", 0)
        self.reach(1, 0)
        self.add("swap", 0)
        self.add("z", 1, 2, 0)
        self.add("prepare", 0)
        zero, one, two, far = [], [], [], []
        for c in range(CHUNKS):
            zero.append(self.solve((0, c, 1)))
            self.send(zero[-1], (0, 1, 0, c, 1))
            if c == 0:
                self.reach("last", 0)
            if c == half - 1:
                far.append(self.send(self.join(*zero), (0, 2, 0, 0, half)))
                self.add("z", 1, 2, 1)
        far.append(self.send(self.join(*zero[half:]), (0, 2, 0, half, CHUNKS - half)))
        self.add("stack", 1)
        self.reach(2, 0)
        self.add("swap", 1)
        self.add("z", 2, 2, 0)
        self.add("prepare", 1)
        for c in range(CHUNKS):
            one.append(self.solve((1, c, 1)))
            self.send(one[-1], (1, 2, 1, c, 1))
            if c == 0:
                self.send(far[0], (2, 3, 0, 0, half))
                self.add("z", "last", 2, 0)
                self.add("z", 2, 2, 1)
            if c == half - 1:
                self.send(self.join(*one), (1, 3, 1, 0, half))
            if c == half:
                near = [self.arrived[1, 0, at][0] for at in range(half, CHUNKS)]
                self.send(self.join(*near), (1, 3, 0, half, CHUNKS - half))
                self.add("z", "last", 2, 1)
                self.pack(2)
        self.send(self.join(*one[half:]), (1, 3, 1, half, CHUNKS - half))
        for c in range(half):
            self.send(self.solve((2, c, 1)), (2, 3, 2, c, 1))
        self.pack("last")
        for c in range(half, CHUNKS):
            self.send(self.solve((2, c, 1)), (2, 3, 2, c, 1))
        early = self.solve((3, 0, half), only=(0, 1))
        self.solve((3, 0, half), base=early, done=(0, 1))
        late = [self.solve((3, c, 1), only=(0, 1)) for c in range(half, CHUNKS)]
        for c, base in zip(range(half, CHUNKS), late):
            self.solve((3, c, 1), base=base, done=(0, 1))

    def many(self):
        last, half = self.last, CHUNKS // 2
        self.add("turn")
        self.add("split")
        self.reach(0)
        self.reach(1)
        self.pack(0)
        for slot in range(CHUNKS + LAG * (last - 1)):
            d, extra = divmod(slot, LAG)
            if extra == 0 and 0 < d < last:
                if d == 1:
                    for far in range(2, last):
                        self.reach(far)
                self.pack(d)
            units = [(r, slot - LAG * r, 1) for r in range(last) if 0 <= slot - LAG * r < CHUNKS]
            key = self.solve(*units)
            for d in range(1, last):
                moves = [(r, r + d, r, c, 1) for r, c, _ in units if r + d < last or d == 1]
                if moves:
                    self.send(key, *moves)
            for r, c, _ in units:
                if r < last - 1 and (c + 1) % half == 0:
                    keys = [key for _, _, key in self.solved[r][-half:]]
                    self.send(self.join(*keys), (r, last, r, c + 1 - half, half))
        self.reach("last")
        self.pack("last")
        for first in (0, half):
            early = self.solve((last, first, half), only=range(last - 1))
            self.solve((last, first, half), base=early, done=range(last - 1))


def whole():
    return pl.BlockSpec(memory_space=pltpu.VMEM)


def body(plan, factor, inverses, right_side):
    return solve(plan, factor, inverses, right_side)


def solve(plan, factor, inverses, right_side):
    block, columns = right_side.shape
    per_block, panel, _ = inverses.shape
    rows, lanes, last = plan.rows, plan.lanes, plan.last
    row = lax.axis_index("row").astype(jnp.int32)
    lane = lax.axis_index("rhs").astype(jnp.int32)
    slices = jnp.transpose(factor, (1, 2, 0))
    width = slices.shape[1]
    piece = columns // CHUNKS
    scalar = pl.BlockSpec(memory_space=pltpu.SMEM)
    half = jax.ShapeDtypeStruct
    grant = pltpu.CompilerParams(vmem_limit_bytes=GRANT)
    where = row.reshape(1)

    def call(kernel, shapes, scalars, values):
        return pl.pallas_call(
            kernel, out_shape=shapes, in_specs=[scalar] * len(scalars) + [whole()] * len(values), compiler_params=grant
        )(*scalars, *values)

    def send(value, moves):
        pairs = [(a * lanes + b, c * lanes + d) for (a, b), (c, d) in moves]
        return lax.ppermute(value, ("row", "rhs"), pairs)

    def users(name):
        return [last] if name == "last" else range(name, rows if name == 0 else last)

    shared = {}
    masks = [0]
    for level in range(lanes.bit_length() - 2):
        masks += [mask ^ (lanes >> (level + 1)) for mask in masks]
    tiles = {}
    parts = {}
    for name in [*range(last), "last"]:
        if name == "last":
            own = slices[: last * per_block]
        elif name == 0:
            own = lax.dynamic_slice_in_dim(slices, row * per_block, per_block - 1, 0)[:, :, panel:]
        else:
            own = lax.dynamic_slice_in_dim(slices, jnp.maximum(row - name, 0) * per_block, per_block, 0)
        parts[name] = {0: own}
    stacked, swapped, values = {}, {}, {}

    def run(step):
        kind, *at = step
        if kind == "z":
            name, bit, index = at
            moves = [((r, q), (r, q ^ bit)) for r in users(name) for q in range(lanes)]
            parts[name][masks[index] ^ bit] = send(parts[name][masks[index]], moves)
        elif kind == "turn":
            values["residual"] = call(turn_kernel, half((columns, block), jnp.float32), [], [right_side])
        elif kind == "split":
            inv = call(split_kernel, [half(inverses.shape, jnp.bfloat16)] * 2, [], [inverses])
            shared.update(inv_high=inv[0], inv_low=inv[1])
        elif kind == "stack":
            mine = [parts[at[0]][mask] for mask in masks]
            shape = half((len(mine), *mine[0].shape), jnp.float32)
            stacked[at[0]] = call(stack_kernel, shape, [], mine)
        elif kind == "swap":
            moves = [((r, q), (r, q ^ 1)) for r in users(at[0]) for q in range(lanes)]
            swapped[at[0]] = send(stacked[at[0]], moves)
        elif kind == "prepare":
            name = at[0]
            mine = [parts[name][mask] for mask in masks]
            count, _, wide = mine[0].shape
            shape = half((count, width * lanes, wide), jnp.bfloat16)
            pair = call(functools.partial(prepare_kernel, masks), [shape] * 2, [lane.reshape(1)], [*mine, swapped[name]])
            for form, value in zip(("high", "low"), pair):
                if name == "last":
                    for g in range(last):
                        tiles["last", last - g, form] = value[g * per_block : (g + 1) * per_block].reshape(-1, wide)
                elif name == 0:
                    shared["own", form] = value.reshape(-1, wide)
                else:
                    tiles["near", name, form] = value.reshape(-1, wide)
        elif kind == "join":
            shape = half((sum(values[key].shape[0] for key in at), block), jnp.float32)
            values[step] = call(join_kernel, shape, [], [values[key] for key in at])
        elif kind == "send":
            key, pairs = at
            values[step] = send(values[key], [((a, q), (b, q)) for a, b in pairs for q in range(lanes)])
        elif kind == "solve":
            count, jobs, base, finish = at
            operands = dict(shared) if finish else {}
            if base is not None:
                operands[base] = values[base]
            layout = []
            for r, first, terms in jobs:
                made = []
                for spot, key, offset, length, distance in terms:
                    pair = ("last" if r == last else "near", distance)
                    operands[key] = values[key]
                    for form in ("high", "low"):
                        operands[pair + (form,)] = tiles[pair + (form,)]
                    made.append((spot * piece, key, offset * piece, length * piece, pair))
                layout.append((r, first * piece, base, made))
            values[step] = call(
                functools.partial(solve_kernel, (list(operands), layout, finish)),
                half((count * piece, block), jnp.float32),
                [where],
                [values["residual"], *operands.values()],
            )

    for step in plan.steps:
        run(step)

    keys = list(dict.fromkeys(key for parts in plan.solved.values() for _, _, key in parts))
    segments = [[(first * piece, count * piece, key) for first, count, key in plan.solved[r]] for r in range(rows)]
    return pl.pallas_call(
        functools.partial(place_kernel, keys, segments),
        out_shape=half((block, columns), jnp.float32),
        in_specs=[scalar] + [pl.BlockSpec(memory_space=pl.ANY)] * len(keys),
        scratch_shapes=[pltpu.VMEM((columns, block), jnp.float32), pltpu.SemaphoreType.DMA((CHUNKS,))],
        compiler_params=grant,
        name="place",
    )(where, *[values[key] for key in keys])


def solution(mesh):
    placed = (P("row", None, "rhs"), P("row", None, None), P("row", "rhs"))
    plan = Plan(mesh.shape["row"], mesh.shape["rhs"])
    return jax.shard_map(
        functools.partial(body, plan), mesh=mesh, in_specs=placed, out_specs=P("row", "rhs"), check_vma=False
    )
```

time: 418 us -> 216 us (0.52)
  the two profiles are of different devices: /device:TPU:0 before, /device:TPU:6 now
where the time goes in v1:
time: 216 us; the launch traced here: 215 us
  waiting for transfers between devices  127 us (59%)
  starting transfers between devices  44.3 us (21%)
  Pallas kernels  32.3 us (15%)
  local copies, waits for them, and re-layouts  10.2 us (5%)
    ppermute x34, waiting for transfers between devices, send(): return lax.ppermute(value, ('row', 'rhs'), pairs)  127 us
    ppermute x34, starting transfers between devices, send(): return lax.ppermute(value, ('row', 'rhs'), pairs)  44.3 us
    pallas_call x33, Pallas kernels, call(): pl.pallas_call(kernel, out_shape=shapes, in_specs=[scalar] * len(scalars)...  30.2 us
    unnamed x44, local copies, waits for them, and re-layouts  5.4 us
  transfers between devices with their start and end apart: 34, of which 11 were waited for; matrix products, arithmetic and copies ran while one was open for 2% of the time, Pallas kernels for 12%

profile of v1, /device:TPU:6, one launch (start us, length us, event | category | flops | bytes accessed | tf_op | source)
XLA Modules:
  0.0 215.0 jit_solution(12069170595451802630)
XLA Ops:
  0.0 1.2 slice.33.refs_0_
  1.2 4.5 %collective-permute-start.23 = (f32[9,32,768]{2,1,0:T(8,128)S(1)}, f32[9,32,768]{2,1,0:T(8,128)S(1)}, u32[]{:S(2)}, u32[]{:S(2)}) collective-permute-start(f32[9,32,768]{2,1,0:T(8,128)S(1)} %slice.33.refs_0_), channel_id=1, source_target_pairs={{24,28},{25,29},{26,30},{27,31},{28,24},{29,25},{30,26},{31,27}} | collective-permute-start | bytes 2654216 | tf_op jit(solution)/shard_map/ppermute | solution.py:280
  5.7 3.5 %collective-permute-start.24 = (f32[9,32,768]{2,1,0:T(8,128)S(1)}, f32[9,32,768]{2,1,0:T(8,128)S(1)}, u32[]{:S(2)}, u32[]{:S(2)}) collective-permute-start(f32[9,32,768]{2,1,0:T(8,128)S(1)} %slice.33.refs_0_), channel_id=1, source_target_pairs={{24,26},{25,27},{26,24},{27,25},{28,30},{29,31},{30,28},{31,29}} | collective-permute-start | bytes 2654216 | tf_op jit(solution)/shard_map/ppermute | solution.py:280
  9.2 35.2 %collective-permute-done.23.refs_1_ = f32[9,32,768]{2,1,0:T(8,128)S(1)} collective-permute-done((f32[9,32,768]{2,1,0:T(8,128)S(1)}, f32[9,32,768]{2,1,0:T(8,128)S(1)}, u32[]{:S(2)}, u32[]{:S(2)}) %collective-permute-start.23) | collective-permute-done | bytes 884768 | tf_op jit(solution)/shard_map/ppermute | solution.py:280
  44.5 2.5 %collective-permute-start.25 = (f32[9,32,768]{2,1,0:T(8,128)S(1)}, f32[9,32,768]{2,1,0:T(8,128)S(1)}, u32[]{:S(2)}, u32[]{:S(2)}) collective-permute-start(f32[9,32,768]{2,1,0:T(8,128)S(1)} %collective-permute-done.23.refs_1_), channel_id=1, source_target_pairs={{24,26},{25,27},{26,24},{27,25},{28,30},{29,31},{30,28},{31,29}} | collective-permute-start | bytes 2654216 | tf_op jit(solution)/shard_map/ppermute | solution.py:280
  47.0 19.9 %collective-permute-done.25.refs_3_ = f32[9,32,768]{2,1,0:T(8,128)S(1)} collective-permute-done((f32[9,32,768]{2,1,0:T(8,128)S(1)}, f32[9,32,768]{2,1,0:T(8,128)S(1)}, u32[]{:S(2)}, u32[]{:S(2)}) %collective-permute-start.25) | collective-permute-done | bytes 884768 | tf_op jit(solution)/shard_map/ppermute | solution.py:280
  66.9 2.0 shard_map.59
  68.8 1.9 collective-permute-start.26
  70.8 1.9 dynamic-slice_bitcast_fusion
  72.7 1.4 collective-permute-start.5
  74.1 0.9 dynamic-slice_bitcast_fusion.2
  75.1 3.4 %collective-permute-start = (f32[2,32,512]{2,1,0:T(8,128)S(1)}, f32[2,32,512]{2,1,0:T(8,128)S(1)}, u32[]{:S(2)}, u32[]{:S(2)}) collective-permute-start(f32[2,32,512]{2,1,0:T(8,128)S(1)} %slice.32.refs_0_), channel_id=1, source_target_pairs={{0,4},{1,5},{2,6},{3,7},{4,0},{5,1},{6,2},{7,3},{8,12},{9,13},{10,... | collective-permute-start | bytes 393224 | tf_op jit(solution)/shard_map/ppermute | solution.py:280
  79.8 1.8 collective-permute-start.1
  81.6 3.9 %collective-permute-done.refs_1_ = f32[2,32,512]{2,1,0:T(8,128)S(1)} collective-permute-done((f32[2,32,512]{2,1,0:T(8,128)S(1)}, f32[2,32,512]{2,1,0:T(8,128)S(1)}, u32[]{:S(2)}, u32[]{:S(2)}) %collective-permute-start) | collective-permute-done | bytes 131104 | tf_op jit(solution)/shard_map/ppermute | solution.py:280
  87.1 3.7 %collective-permute-done.2.refs_3_ = f32[2,32,512]{2,1,0:T(8,128)S(1)} collective-permute-done((f32[2,32,512]{2,1,0:T(8,128)S(1)}, f32[2,32,512]{2,1,0:T(8,128)S(1)}, u32[]{:S(2)}, u32[]{:S(2)}) %collective-permute-start.2) | collective-permute-done | bytes 131104 | tf_op jit(solution)/shard_map/ppermute | solution.py:280
  91.7 2.3 %shard_map.45 = f32[4,3,32,768]{3,2,1,0:T(8,128)} custom-call(f32[3,32,768]{2,1,0:T(8,128)} %get-tuple-element.32.refs_0_, f32[3,32,768]{2,1,0:T(8,128)} %collective-permute-done.5.refs_1_, f32[3,32,768]{2,1,0:T(8,128)S(1)} %collective-permute-done.6.refs_2_, f32[3,32,768]{2,1,0:T(8,128)S(1)} %collective-permute-done.7.refs_3_), custom_call_target="tpu_custom_call" | custom-call | tf_op jit(solution)/shard_map/pallas_call | solution.py:274
  94.1 1.8 collective-permute-start.8
  95.8 1.4 collective-permute-start.13
  97.2 1.4 collective-permute-start.14
  98.6 1.4 copy-done.6
  101.3 1.2 shard_map.40
  105.3 1.2 shard_map.52
  109.8 1.8 shard_map.46
  113.2 1.3 collective-permute-start.30
  114.5 1.3 collective-permute-start.31
  117.4 1.5 shard_map.53
  119.0 1.3 collective-permute-start.33
  120.3 0.9 shard_map.61
  121.3 1.3 collective-permute-start.22
  122.6 1.3 collective-permute-start.27
  126.1 2.9 %shard_map.60 = (bf16[9,256,768]{2,1,0:T(8,128)(2,1)S(1)}, bf16[9,256,768]{2,1,0:T(8,128)(2,1)S(1)}) custom-call(s32[1]{0:T(128)} %bitcast.1.place, f32[9,32,768]{2,1,0:T(8,128)S(1)} %slice.33.refs_0_, f32[9,32,768]{2,1,0:T(8,128)S(1)} %collective-permute-done.23.refs_1_, f32[9,32,768]{2,1,0:T(8,128)S(1)} %collective-permute-done.24.refs_2_, ...), custom_call_target="tpu_custom_call" | custom-call | tf_op jit(solution)/shard_map/pallas_call | solution.py:274
  129.1 14.3 %collective-permute-done.30.refs_0_ = f32[256,768]{1,0:T(8,128)S(1)} collective-permute-done((f32[256,768]{1,0:T(8,128)S(1)}, f32[256,768]{1,0:T(8,128)S(1)}, u32[]{:S(2)}, u32[]{:S(2)}) %collective-permute-start.30) | collective-permute-done | bytes 786464 | tf_op jit(solution)/shard_map/ppermute | solution.py:280
  143.4 0.9 copy-done
  144.3 1.3 collective-permute-start.32
  145.6 12.9 %collective-permute-done.31.refs_3_ = f32[256,768]{1,0:T(8,128)S(1)} collective-permute-done((f32[256,768]{1,0:T(8,128)S(1)}, f32[256,768]{1,0:T(8,128)S(1)}, u32[]{:S(2)}, u32[]{:S(2)}) %collective-permute-start.31) | collective-permute-done | bytes 786464 | tf_op jit(solution)/shard_map/ppermute | solution.py:280
  159.3 1.3 collective-permute-start.29
  160.6 6.8 %collective-permute-done.33.refs_5_ = f32[128,768]{1,0:T(8,128)S(1)} collective-permute-done((f32[128,768]{1,0:T(8,128)S(1)}, f32[128,768]{1,0:T(8,128)S(1)}, u32[]{:S(2)}, u32[]{:S(2)}) %collective-permute-start.33) | collective-permute-done | bytes 393248 | tf_op jit(solution)/shard_map/ppermute | solution.py:280
  168.1 1.3 collective-permute-start.28
  170.8 1.1 shard_map.68.refs_4_
  171.9 1.3 shard_map.66.refs_4_
  173.2 1.9 shard_map.69.refs_14_
  175.1 20.1 %collective-permute-done.32.refs_5_ = f32[128,768]{1,0:T(8,128)S(1)} collective-permute-done((f32[128,768]{1,0:T(8,128)}, f32[128,768]{1,0:T(8,128)S(1)}, u32[]{:S(2)}, u32[]{:S(2)}) %collective-permute-start.32) | collective-permute-done | bytes 393248 | tf_op jit(solution)/shard_map/ppermute | solution.py:280
  195.1 1.8 shard_map.67.refs_13_
  197.0 3.4 %shard_map.62.refs_4_ = f32[256,768]{1,0:T(8,128)S(1)} custom-call(s32[1]{0:T(128)} %bitcast.place, f32[512,768]{1,0:T(8,128)S(1)} %shard_map.37.residual, f32[256,768]{1,0:T(8,128)} %collective-permute-done.22.refs_0_, bf16[768,768]{1,0:T(8,128)(2,1)S(1)} %bitcast.83, bf16[768,768]{1,0:T(8,128)(2,1)S(1)} %bitcast.80, ...), custom_call_target="tpu_custom_call" | custom-call | tf_op jit(solution)/shard_map/pallas_call | solution.py:274
  200.4 3.2 %collective-permute-done.29.refs_8_ = f32[128,768]{1,0:T(8,128)S(1)} collective-permute-done((f32[128,768]{1,0:T(8,128)}, f32[128,768]{1,0:T(8,128)S(1)}, u32[]{:S(2)}, u32[]{:S(2)}) %collective-permute-start.29) | collective-permute-done | bytes 393248 | tf_op jit(solution)/shard_map/ppermute | solution.py:280
  203.6 6.5 %collective-permute-done.28.refs_5_ = f32[128,768]{1,0:T(8,128)S(1)} collective-permute-done((f32[128,768]{1,0:T(8,128)}, f32[128,768]{1,0:T(8,128)S(1)}, u32[]{:S(2)}, u32[]{:S(2)}) %collective-permute-start.28) | collective-permute-done | bytes 393248 | tf_op jit(solution)/shard_map/ppermute | solution.py:280
  210.1 2.6 %shard_map.63.refs_12_ = f32[256,768]{1,0:T(8,128)S(1)} custom-call(s32[1]{0:T(128)} %bitcast.place, f32[512,768]{1,0:T(8,128)S(1)} %shard_map.37.residual, bf16[3,256,256]{2,1,0:T(8,128)(2,1)S(1)} %get-tuple-element.15.refs_0_, bf16[3,256,256]{2,1,0:T(8,128)(2,1)S(1)} %get-tuple-element.16.refs_1_, bf16[512,512]{1,0:T(8,128)(2,1)S(1)} %bitcast.35, ...), custom_call_target="tpu_custom_call" | custom-call | tf_op jit(solution)/shard_map/pallas_call | solution.py:274
  212.7 2.1 place.1
  (103 shorter events, 19.3 us)
Async XLA Ops:
  1.2 43.2 %collective-permute-start.23 = (f32[9,32,768]{2,1,0:T(8,128)S(1)}, f32[9,32,768]{2,1,0:T(8,128)S(1)}, u32[]{:S(2)}, u32[]{:S(2)}) collective-permute-start(f32[9,32,768]{2,1,0:T(8,128)S(1)} %slice.33.refs_0_), channel_id=1, source_target_pairs={{24,28},{25,29},{26,30},{27,31},{28,24},{29,25},{30,26},{31,27}} | collective-permute-start | bytes 2654216 | tf_op jit(solution)/shard_map/ppermute | solution.py:280
  5.7 41.3 %collective-permute-start.24 = (f32[9,32,768]{2,1,0:T(8,128)S(1)}, f32[9,32,768]{2,1,0:T(8,128)S(1)}, u32[]{:S(2)}, u32[]{:S(2)}) collective-permute-start(f32[9,32,768]{2,1,0:T(8,128)S(1)} %slice.33.refs_0_), channel_id=1, source_target_pairs={{24,26},{25,27},{26,24},{27,25},{28,30},{29,31},{30,28},{31,29}} | collective-permute-start | bytes 2654216 | tf_op jit(solution)/shard_map/ppermute | solution.py:280
  44.5 22.4 %collective-permute-start.25 = (f32[9,32,768]{2,1,0:T(8,128)S(1)}, f32[9,32,768]{2,1,0:T(8,128)S(1)}, u32[]{:S(2)}, u32[]{:S(2)}) collective-permute-start(f32[9,32,768]{2,1,0:T(8,128)S(1)} %collective-permute-done.23.refs_1_), channel_id=1, source_target_pairs={{24,26},{25,27},{26,24},{27,25},{28,30},{29,31},{30,28},{31,29}} | collective-permute-start | bytes 2654216 | tf_op jit(solution)/shard_map/ppermute | solution.py:280
  68.8 53.7 %collective-permute-start.26 = (f32[4,9,32,768]{3,2,1,0:T(8,128)}, f32[4,9,32,768]{3,2,1,0:T(8,128)}, u32[]{:S(2)}, u32[]{:S(2)}) collective-permute-start(f32[4,9,32,768]{3,2,1,0:T(8,128)} %shard_map.59), channel_id=1, source_target_pairs={{24,25},{25,24},{26,27},{27,26},{28,29},{29,28},{30,31},{31,30}} | collective-permute-start | bytes 10616840 | tf_op jit(solution)/shard_map/ppermute | solution.py:280
  72.7 6.4 %collective-permute-start.5 = (f32[3,32,768]{2,1,0:T(8,128)}, f32[3,32,768]{2,1,0:T(8,128)}, u32[]{:S(2)}, u32[]{:S(2)}) collective-permute-start(f32[3,32,768]{2,1,0:T(8,128)} %get-tuple-element.32.refs_0_), channel_id=1, source_target_pairs={{8,12},{9,13},{10,14},{11,15},{12,8},{13,9},{14,10},{15,11},{16,20... | collective-permute-start | bytes 884744 | tf_op jit(solution)/shard_map/ppermute | solution.py:280
  75.1 19.0 %copy-start.11 = (f32[2,32,512]{2,1,0:T(8,128)}, f32[2,32,512]{2,1,0:T(8,128)S(1)}, u32[]{:S(2)}) copy-start(f32[2,32,512]{2,1,0:T(8,128)S(1)} %slice.32.refs_0_) | copy-start | bytes 393220
  75.1 10.5 %collective-permute-start = (f32[2,32,512]{2,1,0:T(8,128)S(1)}, f32[2,32,512]{2,1,0:T(8,128)S(1)}, u32[]{:S(2)}, u32[]{:S(2)}) collective-permute-start(f32[2,32,512]{2,1,0:T(8,128)S(1)} %slice.32.refs_0_), channel_id=1, source_target_pairs={{0,4},{1,5},{2,6},{3,7},{4,0},{5,1},{6,2},{7,3},{8,12},{9,13},{10,... | collective-permute-start | bytes 393224 | tf_op jit(solution)/shard_map/ppermute | solution.py:280
  78.5 13.2 %collective-permute-start.6 = (f32[3,32,768]{2,1,0:T(8,128)}, f32[3,32,768]{2,1,0:T(8,128)S(1)}, u32[]{:S(2)}, u32[]{:S(2)}) collective-permute-start(f32[3,32,768]{2,1,0:T(8,128)} %get-tuple-element.32.refs_0_), channel_id=1, source_target_pairs={{8,10},{9,11},{10,8},{11,9},{12,14},{13,15},{14,12},{15,13},{16,18... | collective-permute-start | bytes 884744 | tf_op jit(solution)/shard_map/ppermute | solution.py:280
  79.2 12.5 %collective-permute-start.7 = (f32[3,32,768]{2,1,0:T(8,128)}, f32[3,32,768]{2,1,0:T(8,128)S(1)}, u32[]{:S(2)}, u32[]{:S(2)}) collective-permute-start(f32[3,32,768]{2,1,0:T(8,128)} %collective-permute-done.5.refs_1_), channel_id=1, source_target_pairs={{8,10},{9,11},{10,8},{11,9},{12,14},{13,15},{14,12},{15,13},{16,18... | collective-permute-start | bytes 884744 | tf_op jit(solution)/shard_map/ppermute | solution.py:280
  79.8 7.2 %collective-permute-start.1 = (f32[2,32,512]{2,1,0:T(8,128)S(1)}, f32[2,32,512]{2,1,0:T(8,128)S(1)}, u32[]{:S(2)}, u32[]{:S(2)}) collective-permute-start(f32[2,32,512]{2,1,0:T(8,128)S(1)} %slice.32.refs_0_), channel_id=1, source_target_pairs={{0,2},{1,3},{2,0},{3,1},{4,6},{5,7},{6,4},{7,5},{8,10},{9,11},{10,... | collective-permute-start | bytes 393224 | tf_op jit(solution)/shard_map/ppermute | solution.py:280
  85.5 6.1 %copy-start.14 = (f32[2,32,512]{2,1,0:T(8,128)}, f32[2,32,512]{2,1,0:T(8,128)S(1)}, u32[]{:S(2)}) copy-start(f32[2,32,512]{2,1,0:T(8,128)S(1)} %collective-permute-done.refs_1_) | copy-start | bytes 393220
  85.5 5.3 %collective-permute-start.2 = (f32[2,32,512]{2,1,0:T(8,128)S(1)}, f32[2,32,512]{2,1,0:T(8,128)S(1)}, u32[]{:S(2)}, u32[]{:S(2)}) collective-permute-start(f32[2,32,512]{2,1,0:T(8,128)S(1)} %collective-permute-done.refs_1_), channel_id=1, source_target_pairs={{0,2},{1,3},{2,0},{3,1},{4,6},{5,7},{6,4},{7,5},{8,10},{9,11},{10,... | collective-permute-start | bytes 393224 | tf_op jit(solution)/shard_map/ppermute | solution.py:280
  87.1 4.6 %copy-start.16 = (f32[2,32,512]{2,1,0:T(8,128)}, f32[2,32,512]{2,1,0:T(8,128)S(1)}, u32[]{:S(2)}) copy-start(f32[2,32,512]{2,1,0:T(8,128)S(1)} %collective-permute-done.1.refs_2_) | copy-start | bytes 393220
  91.7 9.6 %collective-permute-start.3 = (f32[4,2,32,512]{3,2,1,0:T(8,128)}, f32[4,2,32,512]{3,2,1,0:T(8,128)}, u32[]{:S(2)}, u32[]{:S(2)}) collective-permute-start(f32[4,2,32,512]{3,2,1,0:T(8,128)} %shard_map.39), channel_id=1, source_target_pairs={{0,1},{1,0},{2,3},{3,2},{4,5},{5,4},{6,7},{7,6},{8,9},{9,8},{10,11... | collective-permute-start | bytes 1572872 | tf_op jit(solution)/shard_map/ppermute | solution.py:280
  91.7 2.4 %copy-start.7 = (f32[3,32,768]{2,1,0:T(8,128)}, f32[3,32,768]{2,1,0:T(8,128)S(1)}, u32[]{:S(2)}) copy-start(f32[3,32,768]{2,1,0:T(8,128)S(1)} %collective-permute-done.6.refs_2_) | copy-start | bytes 884740
  91.7 2.4 %copy-start.9 = (f32[3,32,768]{2,1,0:T(8,128)}, f32[3,32,768]{2,1,0:T(8,128)S(1)}, u32[]{:S(2)}) copy-start(f32[3,32,768]{2,1,0:T(8,128)S(1)} %collective-permute-done.7.refs_3_) | copy-start | bytes 884740
  94.1 15.0 %collective-permute-start.8 = (f32[4,3,32,768]{3,2,1,0:T(8,128)}, f32[4,3,32,768]{3,2,1,0:T(8,128)}, u32[]{:S(2)}, u32[]{:S(2)}) collective-permute-start(f32[4,3,32,768]{3,2,1,0:T(8,128)} %shard_map.45), channel_id=1, source_target_pairs={{8,9},{9,8},{10,11},{11,10},{12,13},{13,12},{14,15},{15,14},{16,17... | collective-permute-start | bytes 3538952 | tf_op jit(solution)/shard_map/ppermute | solution.py:280
  95.8 7.4 %collective-permute-start.13 = (f32[3,32,768]{2,1,0:T(8,128)}, f32[3,32,768]{2,1,0:T(8,128)}, u32[]{:S(2)}, u32[]{:S(2)}) collective-permute-start(f32[3,32,768]{2,1,0:T(8,128)} %get-tuple-element.31.refs_0_), channel_id=1, source_target_pairs={{16,20},{17,21},{18,22},{19,23},{20,16},{21,17},{22,18},{23,19}} | collective-permute-start | bytes 884744 | tf_op jit(solution)/shard_map/ppermute | solution.py:280
  97.2 6.7 %collective-permute-start.14 = (f32[3,32,768]{2,1,0:T(8,128)}, f32[3,32,768]{2,1,0:T(8,128)}, u32[]{:S(2)}, u32[]{:S(2)}) collective-permute-start(f32[3,32,768]{2,1,0:T(8,128)} %get-tuple-element.31.refs_0_), channel_id=1, source_target_pairs={{16,18},{17,19},{18,16},{19,17},{20,22},{21,23},{22,20},{23,21}} | collective-permute-start | bytes 884744 | tf_op jit(solution)/shard_map/ppermute | solution.py:280
  98.6 1.4 copy-start.6
  100.0 1.3 copy-start.17
  100.0 1.3 copy-start.19
  102.5 4.1 %collective-permute-start.11 = (f32[128,768]{1,0:T(8,128)S(1)}, f32[128,768]{1,0:T(8,128)S(1)}, u32[]{:S(2)}, u32[]{:S(2)}) collective-permute-start(f32[128,768]{1,0:T(8,128)S(1)} %shard_map.44.refs_1_.refs_3_), channel_id=1, source_target_pairs={{0,8},{1,9},{2,10},{3,11},{4,12},{5,13},{6,14},{7,15}} | collective-permute-start | bytes 1179656 | tf_op jit(solution)/shard_map/ppermute | solution.py:280
  103.2 4.2 %collective-permute-start.10 = (f32[128,768]{1,0:T(8,128)S(1)}, f32[128,768]{1,0:T(8,128)S(1)}, u32[]{:S(2)}, u32[]{:S(2)}) collective-permute-start(f32[128,768]{1,0:T(8,128)S(1)} %shard_map.43.refs_0_.refs_2_), channel_id=1, source_target_pairs={{0,8},{1,9},{2,10},{3,11},{4,12},{5,13},{6,14},{7,15}} | collective-permute-start | bytes 1179656 | tf_op jit(solution)/shard_map/ppermute | solution.py:280
  103.9 0.7 collective-permute-start.15
  104.6 3.6 %collective-permute-start.9 = (f32[128,768]{1,0:T(8,128)S(1)}, f32[128,768]{1,0:T(8,128)S(1)}, u32[]{:S(2)}, u32[]{:S(2)}) collective-permute-start(f32[128,768]{1,0:T(8,128)S(1)} %shard_map.42.refs_1_), channel_id=1, source_target_pairs={{0,8},{1,9},{2,10},{3,11},{4,12},{5,13},{6,14},{7,15}} | collective-permute-start | bytes 1179656 | tf_op jit(solution)/shard_map/ppermute | solution.py:280
  106.6 8.0 %collective-permute-start.16 = (f32[4,3,32,768]{3,2,1,0:T(8,128)S(1)}, f32[4,3,32,768]{3,2,1,0:T(8,128)S(1)}, u32[]{:S(2)}, u32[]{:S(2)}) collective-permute-start(f32[4,3,32,768]{3,2,1,0:T(8,128)S(1)} %shard_map.52), channel_id=1, source_target_pairs={{16,17},{17,16},{18,19},{19,18},{20,21},{21,20},{22,23},{23,22}} | collective-permute-start | bytes 3538952 | tf_op jit(solution)/shard_map/ppermute | solution.py:280
  107.4 5.0 %collective-permute-start.19 = (f32[256,768]{1,0:T(8,128)S(1)}, f32[256,768]{1,0:T(8,128)S(1)}, u32[]{:S(2)}, u32[]{:S(2)}) collective-permute-start(f32[256,768]{1,0:T(8,128)S(1)} %shard_map.56), channel_id=1, source_target_pairs={{0,16},{1,17},{2,18},{3,19},{4,20},{5,21},{6,22},{7,23}} | collective-permute-start | bytes 2359304 | tf_op jit(solution)/shard_map/ppermute | solution.py:280
  108.1 1.6 copy-start.8
  108.1 1.6 copy-start.10
  108.2 5.0 %collective-permute-start.12 = (f32[256,768]{1,0:T(8,128)S(1)}, f32[256,768]{1,0:T(8,128)S(1)}, u32[]{:S(2)}, u32[]{:S(2)}) collective-permute-start(f32[256,768]{1,0:T(8,128)S(1)} %shard_map.51), channel_id=1, source_target_pairs={{0,16},{1,17},{2,18},{3,19},{4,20},{5,21},{6,22},{7,23}} | collective-permute-start | bytes 2359304 | tf_op jit(solution)/shard_map/ppermute | solution.py:280
  109.1 2.6 %collective-permute-start.4 = (f32[128,768]{1,0:T(8,128)S(1)}, f32[128,768]{1,0:T(8,128)S(1)}, u32[]{:S(2)}, u32[]{:S(2)}) collective-permute-start(f32[128,768]{1,0:T(8,128)S(1)} %shard_map.41.refs_0_), channel_id=1, source_target_pairs={{0,8},{1,9},{2,10},{3,11},{4,12},{5,13},{6,14},{7,15}} | collective-permute-start | bytes 1179656 | tf_op jit(solution)/shard_map/ppermute | solution.py:280
  111.7 4.2 %collective-permute-start.21 = (f32[128,768]{1,0:T(8,128)S(1)}, f32[128,768]{1,0:T(8,128)S(1)}, u32[]{:S(2)}, u32[]{:S(2)}) collective-permute-start(f32[128,768]{1,0:T(8,128)S(1)} %shard_map.50.refs_1_.refs_7_), channel_id=1, source_target_pairs={{8,16},{9,17},{10,18},{11,19},{12,20},{13,21},{14,22},{15,23}} | collective-permute-start | bytes 1179656 | tf_op jit(solution)/shard_map/ppermute | solution.py:280
  112.4 4.4 %collective-permute-start.20 = (f32[128,768]{1,0:T(8,128)S(1)}, f32[128,768]{1,0:T(8,128)S(1)}, u32[]{:S(2)}, u32[]{:S(2)}) collective-permute-start(f32[128,768]{1,0:T(8,128)S(1)} %shard_map.49.refs_0_.refs_6_), channel_id=1, source_target_pairs={{8,16},{9,17},{10,18},{11,19},{12,20},{13,21},{14,22},{15,23}} | collective-permute-start | bytes 1179656 | tf_op jit(solution)/shard_map/ppermute | solution.py:280
  113.2 30.1 %collective-permute-start.30 = (f32[256,768]{1,0:T(8,128)S(1)}, f32[256,768]{1,0:T(8,128)S(1)}, u32[]{:S(2)}, u32[]{:S(2)}) collective-permute-start(f32[256,768]{1,0:T(8,128)S(1)} %shard_map.64), channel_id=1, source_target_pairs={{8,24},{9,25},{10,26},{11,27},{12,28},{13,29},{14,30},{15,31}} | collective-permute-start | bytes 2359304 | tf_op jit(solution)/shard_map/ppermute | solution.py:280
  114.5 43.9 %collective-permute-start.31 = (f32[256,768]{1,0:T(8,128)S(1)}, f32[256,768]{1,0:T(8,128)S(1)}, u32[]{:S(2)}, u32[]{:S(2)}) collective-permute-start(f32[256,768]{1,0:T(8,128)S(1)} %shard_map.65), channel_id=1, source_target_pairs={{8,24},{9,25},{10,26},{11,27},{12,28},{13,29},{14,30},{15,31}} | collective-permute-start | bytes 2359304 | tf_op jit(solution)/shard_map/ppermute | solution.py:280
  115.8 3.2 %collective-permute-start.18 = (f32[128,768]{1,0:T(8,128)S(1)}, f32[128,768]{1,0:T(8,128)S(1)}, u32[]{:S(2)}, u32[]{:S(2)}) collective-permute-start(f32[128,768]{1,0:T(8,128)S(1)} %shard_map.48.refs_1_.refs_5_), channel_id=1, source_target_pairs={{8,16},{9,17},{10,18},{11,19},{12,20},{13,21},{14,22},{15,23}} | collective-permute-start | bytes 1179656 | tf_op jit(solution)/shard_map/ppermute | solution.py:280
  116.8 4.5 %collective-permute-start.17 = (f32[128,768]{1,0:T(8,128)S(1)}, f32[128,768]{1,0:T(8,128)S(1)}, u32[]{:S(2)}, u32[]{:S(2)}) collective-permute-start(f32[128,768]{1,0:T(8,128)S(1)} %shard_map.47.refs_0_.refs_4_), channel_id=1, source_target_pairs={{8,16},{9,17},{10,18},{11,19},{12,20},{13,21},{14,22},{15,23}} | collective-permute-start | bytes 1179656 | tf_op jit(solution)/shard_map/ppermute | solution.py:280
  119.0 5.6 %copy-start.4 = (f32[128,768]{1,0:T(8,128)}, f32[128,768]{1,0:T(8,128)S(1)}, u32[]{:S(2)}) copy-start(f32[128,768]{1,0:T(8,128)S(1)} %shard_map.58.refs_11_) | copy-start | bytes 1179652
  119.0 48.3 %collective-permute-start.33 = (f32[128,768]{1,0:T(8,128)S(1)}, f32[128,768]{1,0:T(8,128)S(1)}, u32[]{:S(2)}, u32[]{:S(2)}) collective-permute-start(f32[128,768]{1,0:T(8,128)S(1)} %shard_map.58.refs_11_), channel_id=1, source_target_pairs={{16,24},{17,25},{18,26},{19,27},{20,28},{21,29},{22,30},{23,31}} | collective-permute-start | bytes 1179656 | tf_op jit(solution)/shard_map/ppermute | solution.py:280
  121.3 75.7 %collective-permute-start.22 = (f32[256,768]{1,0:T(8,128)S(1)}, f32[256,768]{1,0:T(8,128)}, u32[]{:S(2)}, u32[]{:S(2)}) collective-permute-start(f32[256,768]{1,0:T(8,128)S(1)} %collective-permute-done.12.refs_4_), channel_id=1, source_target_pairs={{16,24},{17,25},{18,26},{19,27},{20,28},{21,29},{22,30},{23,31}} | collective-permute-start | bytes 2359304 | tf_op jit(solution)/shard_map/ppermute | solution.py:280
  122.6 74.4 %collective-permute-start.27 = (f32[256,768]{1,0:T(8,128)}, f32[256,768]{1,0:T(8,128)}, u32[]{:S(2)}, u32[]{:S(2)}) collective-permute-start(f32[256,768]{1,0:T(8,128)} %shard_map.61), channel_id=1, source_target_pairs={{8,24},{9,25},{10,26},{11,27},{12,28},{13,29},{14,30},{15,31}} | collective-permute-start | bytes 2359304 | tf_op jit(solution)/shard_map/ppermute | solution.py:280
  144.3 50.9 %collective-permute-start.32 = (f32[128,768]{1,0:T(8,128)}, f32[128,768]{1,0:T(8,128)S(1)}, u32[]{:S(2)}, u32[]{:S(2)}) collective-permute-start(f32[128,768]{1,0:T(8,128)} %shard_map.57.refs_10_), channel_id=1, source_target_pairs={{16,24},{17,25},{18,26},{19,27},{20,28},{21,29},{22,30},{23,31}} | collective-permute-start | bytes 1179656 | tf_op jit(solution)/shard_map/ppermute | solution.py:280
  159.3 44.3 %collective-permute-start.29 = (f32[128,768]{1,0:T(8,128)}, f32[128,768]{1,0:T(8,128)S(1)}, u32[]{:S(2)}, u32[]{:S(2)}) collective-permute-start(f32[128,768]{1,0:T(8,128)} %shard_map.55.refs_9_), channel_id=1, source_target_pairs={{16,24},{17,25},{18,26},{19,27},{20,28},{21,29},{22,30},{23,31}} | collective-permute-start | bytes 1179656 | tf_op jit(solution)/shard_map/ppermute | solution.py:280
  168.1 42.0 %collective-permute-start.28 = (f32[128,768]{1,0:T(8,128)}, f32[128,768]{1,0:T(8,128)S(1)}, u32[]{:S(2)}, u32[]{:S(2)}) collective-permute-start(f32[128,768]{1,0:T(8,128)} %shard_map.54.refs_8_), channel_id=1, source_target_pairs={{16,24},{17,25},{18,26},{19,27},{20,28},{21,29},{22,30},{23,31}} | collective-permute-start | bytes 1179656 | tf_op jit(solution)/shard_map/ppermute | solution.py:280
  169.4 1.4 copy-start.3
  171.9 1.3 copy-start.21
  200.4 12.3 %copy-start.5 = (f32[128,768]{1,0:T(8,128)S(1)}, f32[128,768]{1,0:T(8,128)}, u32[]{:S(2)}) copy-start(f32[128,768]{1,0:T(8,128)} %copy-done.4) | copy-start | bytes 1179652
  (8 other events, 8.3 us)
